TPU v7x, 32 devices: a whole 2x2x4 slice. The times are simulated.
32 devices in a mesh: kpt: 4 (over y, x), grid: 8 (over z, core).
Axes of the slice: x: 2, y: 2, z: 4, core: 2. Of those that a mesh axis runs over, the one named last changes fastest.
Arguments:
- bands: float32 [4, 2, 2, 48, 2304], P('kpt', None, None, 'grid'), may hold values from -6 to 6
- potential: float32 [48, 2304], P('grid'), may hold values from -4 to 4
- phase_numerator_table: int32 [4, 3], P('kpt'), may hold values from 0 to 7
- kweight: float32 [4], P('kpt'), may hold values from 0.25 to 2
- lowest: float32 [4], P('kpt'), may hold values from -6 to -4.5
- cut: float32 [4], P('kpt'), may hold values from 0 to 3
- upper: float32 [4], P('kpt'), may hold values from 15 to 17
- fermi: float32 [1], replicated, may hold values from -0.5 to 1.5
Outputs:
- filtered: float32 [4, 2, 2, 48, 2304], P('kpt', None, None, 'grid')
- band_energies: float32 [4, 2], P('kpt')
- total_energy: float32 [1], replicated
All inputs are finite; a program needn't handle non-finite values.
Results may differ from a plain program's by a relative error of at most 0.00022.
Values sent between devices are 32-bit elements; how exact they have to be, the bound alone decides.
A program may use at most 128 MiB of HBM per device.

v0:
```python
import functools

import jax
import jax.numpy as jnp
import numpy as np
from jax import lax
from jax.experimental import pallas as pl
from jax.experimental.pallas import tpu as pltpu
from jax.sharding import PartitionSpec as P

SIDE = 48
DEGREE = 6
PHASE_DIVISOR = 8
REACH = 6
LANES = 128
USED = 2 * SIDE
PAD = 8
ROWS = SIDE + 2 * PAD
HALF = SIDE // 2
TILES = SIDE // 8

coefficients = (
    -5369.0 / 1800.0,
    12.0 / 7.0,
    -15.0 / 56.0,
    10.0 / 189.0,
    -1.0 / 112.0,
    2.0 / 1925.0,
    -1.0 / 16632.0,
)
smearing = 0.5
MESH = pl.DeviceIdType.MESH


def third_parts():
    inside = np.zeros((SIDE, SIDE))
    over = np.zeros((SIDE, SIDE))
    under = np.zeros((SIDE, SIDE))
    for z in range(SIDE):
        for j in range(1, REACH + 1):
            weight = -0.5 * coefficients[j]
            for target, sign in ((z + j, 1), (z - j, -1)):
                if 0 <= target < SIDE:
                    inside[target, z] += weight
                elif sign > 0:
                    over[target - SIDE, z] += weight
                else:
                    under[target + SIDE, z] += weight
    plain = np.zeros((LANES, LANES))
    cosine = np.zeros((LANES, LANES))
    sine = np.zeros((LANES, LANES))
    both, apart = over + under, over - under
    for c in range(2):
        s = slice(c * SIDE, (c + 1) * SIDE)
        plain[s, s] = inside
        cosine[s, s] = both
    re, im = slice(0, SIDE), slice(SIDE, USED)
    sine[im, re] = -apart
    sine[re, im] = apart
    return [a.astype(np.float32) for a in (plain, cosine, sine)]


def kernel(
    n,
    members_k,
    scal_ref,
    packed_ref,
    pot_ref,
    mat_ref,
    out_ref,
    energy_ref,
    total_ref,
    field,
    potential,
    gathered,
    gathered_pot,
    part,
    part_k,
    send,
    recv,
    send_pot,
    recv_pot,
    send_red,
    recv_red,
    send_k,
    recv_k,
    swap_sem,
):
    planes = REACH
    chips = n // 2
    blocks = n
    home = (blocks - 2) // 2
    me = lax.axis_index("grid")
    kpt = lax.axis_index("kpt")
    chip, core = me // 2, me % 2
    partner = chip * 2 + (1 - core)

    barrier = pltpu.get_barrier_semaphore()
    for d in range(1, n):
        pl.semaphore_signal(barrier, inc=1, device_id=(kpt, (me + d) % n), device_id_type=MESH)
    for d in range(1, members_k):
        pl.semaphore_signal(
            barrier, inc=1, device_id=((kpt + d) % members_k, me), device_id_type=MESH
        )
    pl.semaphore_wait(barrier, n - 1 + members_k - 1)

    def remote(src, dst, ssem, rsem, target):
        return pltpu.make_async_remote_copy(
            src_ref=src,
            dst_ref=dst,
            send_sem=ssem,
            recv_sem=rsem,
            device_id=(kpt, target),
            device_id_type=MESH,
        )

    has_up, has_down = chip < chips - 1, chip > 0

    def own(which, ssem, target):
        return remote(packed_ref.at[which], gathered.at[me], ssem, recv.at[me], target)

    def own_pot(ssem, target):
        return remote(pot_ref, gathered_pot.at[me], ssem, recv_pot.at[me], target)

    @pl.when(has_up)
    def _():
        own(core, send.at[0], me + 2).start()
        own(1 - core, send.at[1], partner + 2).start()
        own_pot(send_pot.at[0], me + 2).start()

    @pl.when(has_down)
    def _():
        own(core, send.at[2], me - 2).start()
        own(1 - core, send.at[3], partner - 2).start()
        own_pot(send_pot.at[1], me - 2).start()

    own(1 - core, send.at[4], partner).start()
    own_pot(send_pot.at[2], partner).start()

    lane = lax.broadcasted_iota(jnp.int32, (8, LANES), 1)
    first = lane < SIDE
    used = lane < USED
    zero = jnp.zeros((8, LANES), jnp.float32)

    def turn(v, cosine, sine):
        other = jnp.where(first, pltpu.roll(v, LANES - SIDE, 1), pltpu.roll(v, SIDE, 1))
        signed = jnp.where(used, jnp.where(first, -sine, sine), 0.0)
        return cosine * v + signed * other

    cos_x, sin_x = scal_ref[0], scal_ref[1]
    cos_y, sin_y = scal_ref[2], scal_ref[3]

    def put(slot, plane, t, v):
        field[slot, plane, pl.ds(PAD + 8 * t, 8), :] = v
        if t == 0:
            field[slot, plane, pl.ds(PAD + SIDE, 8), :] = turn(v, cos_y, sin_y)
        if t == TILES - 1:
            field[slot, plane, pl.ds(0, 8), :] = turn(v, cos_y, -sin_y)

    def unpack(load, slab):
        place = lax.rem(slab - 2 * chip + home + blocks, blocks)
        absolute = 2 * chip - home + place
        wrapped_low = absolute < 0
        wrapped_high = absolute >= blocks
        base = planes + place * planes

        def emit(change):
            for hp in range(2 * planes):
                plane, half = hp // 2, hp % 2
                for r in range(HALF // 8):
                    if hp < 9:
                        v = jnp.where(used, load(hp, r), zero)
                    else:
                        g = hp - 9
                        v = zero
                        for q in range(3):
                            piece = pltpu.roll(load(3 * g + q, r), 32 + 32 * q, 1)
                            inside = (lane >= 32 * q) & (lane < 32 * q + 32)
                            v = jnp.where(inside, piece, v)
                    put(0, base + plane, half * (HALF // 8) + r, change(v))

        sine = jnp.where(wrapped_low, -sin_x, sin_x)
        sine = jnp.where(wrapped_low | wrapped_high, sine, 0.0)
        cosine = jnp.where(wrapped_low | wrapped_high, cos_x, 1.0)
        emit(lambda v: turn(v, cosine, sine))

    def unpack_pot(load, slab):
        place = lax.rem(slab - 2 * chip + home + blocks, blocks)
        for pair in range(planes // 2):
            for t in range(TILES):
                v = load(pair, t) - 1.5 * coefficients[0]
                swap_up = pltpu.roll(v, SIDE, 1)
                swap_down = pltpu.roll(v, LANES - SIDE, 1)
                rows = pl.ds(8 * t, 8)
                potential[place * planes + 2 * pair, rows, :] = jnp.where(first, v, swap_up)
                potential[place * planes + 2 * pair + 1, rows, :] = jnp.where(first, swap_down, v)

    def own_load(hp, r):
        return packed_ref[core, hp, pl.ds(8 * r, 8), :]

    unpack(own_load, me)
    unpack_pot(lambda pair, t: pot_ref[pair, pl.ds(8 * t, 8), :], me)

    def unpack_slab(slab):
        unpack(lambda hp, r: gathered[slab, hp, pl.ds(8 * r, 8), :], slab)

    def unpack_pot_slab(slab):
        unpack_pot(lambda pair, t: gathered_pot[slab, pair, pl.ds(8 * t, 8), :], slab)

    def await_slab(slab):
        remote(gathered.at[slab], gathered.at[slab], send.at[0], recv.at[slab], partner).wait_recv()

    def await_pot(slab):
        remote(
            gathered_pot.at[slab], gathered_pot.at[slab], send_pot.at[0], recv_pot.at[slab], partner
        ).wait_recv()

    def relay(slab, target):
        return remote(
            gathered.at[slab], gathered.at[slab], send.at[5 + slab], recv.at[slab], target
        )

    def relay_pot(slab, target, side):
        return remote(
            gathered_pot.at[slab],
            gathered_pot.at[slab],
            send_pot.at[3 + 2 * slab + side],
            recv_pot.at[slab],
            target,
        )

    def arrive(source, onward, target):
        for p in range(2):
            slab = 2 * source + p
            await_slab(slab)

            @pl.when(onward)
            def _():
                relay(slab, target).start()

        same = 2 * source + core
        await_pot(same)

        @pl.when(onward)
        def _():
            relay_pot(same, target, 0).start()

        relay_pot(same, partner, 1).start()

    def process(source):
        def one(p, carry):
            slab = 2 * source + p
            unpack_slab(slab)
            return carry

        lax.fori_loop(0, 2, one, 0)
        unpack_pot_slab(2 * source + core)

    def gather_step(d, carry):
        low_there, high_there = chip - d >= 0, chip + d < chips

        @pl.when(low_there)
        def _():
            arrive(chip - d, has_up, me + 2)

        @pl.when(high_there)
        def _():
            arrive(chip + d, has_down, me - 2)

        @pl.when(low_there)
        def _():
            process(chip - d)

        @pl.when(high_there)
        def _():
            process(chip + d)

        return carry

    await_slab(partner)
    unpack_slab(partner)
    await_pot(partner)
    unpack_pot_slab(partner)
    lax.fori_loop(1, chips, gather_step, 0)

    def other_pot(source, carry):
        @pl.when(source != chip)
        def _():
            slab = 2 * source + (1 - core)
            await_pot(slab)
            unpack_pot_slab(slab)

        return carry

    lax.fori_loop(0, chips, other_pot, 0)

    def wrap_planes(slot):
        def one(i, carry):
            for t in range(ROWS // 8):
                rows = pl.ds(8 * t, 8)
                low = field[slot, blocks * planes + i, rows, :]
                field[slot, i, rows, :] = turn(low, cos_x, -sin_x)
                high = field[slot, planes + i, rows, :]
                field[slot, planes + blocks * planes + i, rows, :] = turn(high, cos_x, sin_x)
            return carry

        lax.fori_loop(0, planes, one, 0)

    wrap_planes(0)
    weights = [-0.5 * c for c in coefficients]

    def step(m, carry):
        now = lax.rem(m - 1, 3)
        new = lax.rem(m, 3)
        old = jnp.where(m == 1, now, lax.rem(m + 1, 3))
        gain, centre, back = scal_ref[3 * m + 1], scal_ref[3 * m + 2], scal_ref[3 * m + 3]
        low = jnp.maximum(0, m - (DEGREE + 1) + home)

        def block(k, inner):
            base = k * planes
            middle = [field[now, base + planes + p, pl.ds(PAD, SIDE), :] for p in range(planes)]
            rows = jnp.concatenate(middle, axis=0)
            high = rows.astype(jnp.bfloat16)
            rest = (rows - high.astype(jnp.float32)).astype(jnp.bfloat16)
            both = jnp.concatenate([high, rest], axis=1)
            third = jnp.dot(both, mat_ref[...], preferred_element_type=jnp.float32)
            third = third[:, :LANES] + third[:, LANES:]
            for t in range(TILES):
                window = [
                    field[now, base + i, pl.ds(PAD + 8 * t, 8), :] for i in range(3 * planes)
                ]
                for p in range(planes):
                    centre_value = window[planes + p]
                    total = third[p * SIDE + 8 * t : p * SIDE + 8 * t + 8, :]
                    total = total + centre_value * (
                        potential[base + p, pl.ds(8 * t, 8), :] - centre
                    )
                    for j in range(1, REACH + 1):
                        around = window[planes + p + j] + window[planes + p - j]
                        above = field[now, base + planes + p, pl.ds(PAD + 8 * t + j, 8), :]
                        below = field[now, base + planes + p, pl.ds(PAD + 8 * t - j, 8), :]
                        total = total + weights[j] * (around + (above + below))
                    previous = field[old, base + planes + p, pl.ds(PAD + 8 * t, 8), :]
                    put(new, base + planes + p, t, gain * total - back * previous)
            return inner

        lax.fori_loop(low, blocks - low, block, 0)

        @pl.when(m - DEGREE + home <= 0)
        def _():
            wrap_planes(new)

        return carry

    lax.fori_loop(1, DEGREE + 2, step, 0)
    slot, applied = DEGREE % 3, (DEGREE + 1) % 3

    mine = planes + (home + core) * planes
    theirs = planes + (home + 1 - core) * planes
    body = pl.ds(PAD, SIDE)
    swap = remote(
        field.at[slot, pl.ds(theirs, planes), body, :],
        out_ref.at[core],
        swap_sem.at[0],
        swap_sem.at[1],
        partner,
    )
    swap.start()

    def sums(i, carry):
        top, bottom = carry
        plane = planes + home * planes + i
        for t in range(TILES):
            f = field[slot, plane, pl.ds(PAD + 8 * t, 8), :]
            top = top + f * field[applied, plane, pl.ds(PAD + 8 * t, 8), :]
            bottom = bottom + f * f
        return top, bottom

    top, bottom = lax.fori_loop(0, 2 * planes, sums, (zero, zero))
    part[me, 0] = jnp.broadcast_to(jnp.sum(top, keepdims=True), (8, LANES))
    part[me, 1] = jnp.broadcast_to(jnp.sum(bottom, keepdims=True), (8, LANES))

    def reduction(d):
        return remote(
            part.at[me], part.at[me], send_red.at[d], recv_red.at[me], lax.rem(me + d, n)
        )

    for d in range(1, n):
        reduction(d).start()
    for i in range(planes):
        for t in range(TILES):
            out_ref[core, i, pl.ds(8 * t, 8), :] = field[slot, mine + i, pl.ds(PAD + 8 * t, 8), :]
    for d in range(1, n):
        source = lax.rem(me + d, n)
        remote(
            part.at[source], part.at[source], send_red.at[d], recv_red.at[source], source
        ).wait_recv()
    kweight, fermi = scal_ref[3 * DEGREE + 7], scal_ref[3 * DEGREE + 8]
    term = zero
    for b in range(2):
        numerator, denominator = zero, zero
        for c in range(chips):
            numerator = numerator + part[2 * c + b, 0]
            denominator = denominator + part[2 * c + b, 1]
        energy = numerator / denominator
        energy_ref[b] = energy
        term = term + energy / (1.0 + jnp.exp((energy - fermi) / smearing))
    part_k[kpt] = kweight * term

    def across(d):
        return pltpu.make_async_remote_copy(
            src_ref=part_k.at[kpt],
            dst_ref=part_k.at[kpt],
            send_sem=send_k.at[d],
            recv_sem=recv_k.at[kpt],
            device_id=(lax.rem(kpt + d, members_k), me),
            device_id_type=MESH,
        )

    for d in range(1, members_k):
        across(d).start()
    for d in range(1, members_k):
        source = lax.rem(kpt + d, members_k)
        pltpu.make_async_remote_copy(
            src_ref=part_k.at[source],
            dst_ref=part_k.at[source],
            send_sem=send_k.at[d],
            recv_sem=recv_k.at[source],
            device_id=(source, me),
            device_id_type=MESH,
        ).wait_recv()
    grand = zero
    for k in range(members_k):
        grand = grand + part_k[k]
    total_ref[...] = grand

    swap.wait()
    for d in range(1, n):
        reduction(d).wait_send()
    for d in range(1, members_k):
        across(d).wait_send()

    @pl.when(has_up)
    def _():
        own(core, send.at[0], me + 2).wait_send()
        own(1 - core, send.at[1], partner + 2).wait_send()
        own_pot(send_pot.at[0], me + 2).wait_send()

    @pl.when(has_down)
    def _():
        own(core, send.at[2], me - 2).wait_send()
        own(1 - core, send.at[3], partner - 2).wait_send()
        own_pot(send_pot.at[1], me - 2).wait_send()

    own(1 - core, send.at[4], partner).wait_send()
    own_pot(send_pot.at[2], partner).wait_send()

    def drain(source, carry):
        @pl.when(source != chip)
        def _():
            onward = jnp.where(source < chip, has_up, has_down)
            target = jnp.where(source < chip, me + 2, me - 2)

            @pl.when(onward)
            def _():
                relay(2 * source, target).wait_send()
                relay(2 * source + 1, target).wait_send()
                relay_pot(2 * source + core, target, 0).wait_send()

            relay_pot(2 * source + core, partner, 1).wait_send()

        return carry

    lax.fori_loop(0, chips, drain, 0)


def per_device(bands, potential, table, kweight, lowest, cut, upper, fermi):
    n = lax.axis_size("grid")
    members_k = lax.axis_size("kpt")
    planes = bands.shape[3]
    angles = 2.0 * jnp.pi * table[0].astype(jnp.float32) / PHASE_DIVISOR
    cosines, sines = jnp.cos(angles), jnp.sin(angles)

    half_width = (upper[0] - cut[0]) / 2.0
    centre = (upper[0] + cut[0]) / 2.0
    first_sigma = half_width / (lowest[0] - centre)
    sigma = first_sigma
    nothing = jnp.zeros((), jnp.float32)
    scalars = [cosines[0], sines[0], cosines[1], sines[1]]
    scalars += [first_sigma / half_width, centre, nothing]
    for degree in range(1, DEGREE):
        next_sigma = 1.0 / (2.0 / first_sigma - sigma)
        scalars += [2.0 * next_sigma / half_width, centre, sigma * next_sigma]
        sigma = next_sigma
    scalars += [nothing + 1.0, nothing, nothing, kweight[0], fermi[0]]
    scalars = jnp.stack(scalars)

    plain, cosine, sine = third_parts()
    matrix = plain + cosines[2] * cosine + sines[2] * sine
    rounded = lax.reduce_precision(matrix, 8, 7)
    high = rounded.astype(jnp.bfloat16)
    rest = (matrix - rounded).astype(jnp.bfloat16)
    matrix = jnp.concatenate(
        [
            jnp.concatenate([high, rest], axis=1),
            jnp.concatenate([high, jnp.zeros_like(high)], axis=1),
        ],
        axis=0,
    )

    waves = bands[0].reshape(2, 2, planes, SIDE, SIDE).transpose(1, 2, 3, 0, 4)
    waves = waves.reshape(2, 2 * planes, HALF, USED)
    head, tail = waves[:, :9], waves[:, 9:]
    tail = tail.reshape(2, 3, HALF, 3, 32).transpose(0, 1, 3, 2, 4).reshape(2, 9, HALF, 32)
    packed = jnp.concatenate([head, tail], axis=-1)

    pairs = potential.reshape(planes // 2, 2, SIDE, SIDE).transpose(0, 2, 1, 3)
    pairs = pairs.reshape(planes // 2, SIDE, USED)
    pairs = jnp.pad(pairs, ((0, 0), (0, 0), (0, LANES - USED)))

    vmem = pl.BlockSpec(memory_space=pltpu.VMEM)
    total_planes = n * planes
    dma = pltpu.SemaphoreType.DMA
    out, energy, total = pl.pallas_call(
        functools.partial(kernel, n, members_k),
        name="cheb",
        out_shape=(
            jax.ShapeDtypeStruct((2, planes, SIDE, LANES), jnp.float32),
            jax.ShapeDtypeStruct((2, 8, LANES), jnp.float32),
            jax.ShapeDtypeStruct((8, LANES), jnp.float32),
        ),
        in_specs=[pl.BlockSpec(memory_space=pltpu.SMEM), vmem, vmem, vmem],
        out_specs=(vmem, vmem, vmem),
        scratch_shapes=[
            pltpu.VMEM((3, total_planes + 2 * planes, ROWS, LANES), jnp.float32),
            pltpu.VMEM((total_planes, SIDE, LANES), jnp.float32),
            pltpu.VMEM((n, 9, HALF, LANES), jnp.float32),
            pltpu.VMEM((n, planes // 2, SIDE, LANES), jnp.float32),
            pltpu.VMEM((n, 2, 8, LANES), jnp.float32),
            pltpu.VMEM((members_k, 8, LANES), jnp.float32),
            dma((5 + n,)),
            dma((n,)),
            dma((3 + 2 * n,)),
            dma((n,)),
            dma((n,)),
            dma((n,)),
            dma((members_k,)),
            dma((members_k,)),
            dma((2,)),
        ],
        compiler_params=pltpu.CompilerParams(
            collective_id=0, has_side_effects=True, vmem_limit_bytes=56 * 1024 * 1024
        ),
    )(scalars, packed, pairs, matrix)
    filtered = out[..., :USED].reshape(2, planes, SIDE, 2, SIDE).transpose(3, 0, 1, 2, 4)
    filtered = filtered.reshape(1, 2, 2, planes, SIDE * SIDE)
    return filtered, energy[:, 0, 0][None], total[0, :1]


def solution(mesh):
    in_specs = (
        P("kpt", None, None, "grid", None),
        P("grid", None),
        P("kpt", None),
        P("kpt"),
        P("kpt"),
        P("kpt"),
        P("kpt"),
        P(),
    )
    out_specs = (P("kpt", None, None, "grid", None), P("kpt", None), P())
    return jax.shard_map(
        per_device, mesh=mesh, in_specs=in_specs, out_specs=out_specs, check_vma=False
    )
```

profile of v0, /device:TPU:0, one launch (start us, length us, event | category | flops | bytes accessed | tf_op | source)
XLA Modules:
  0.0 125.9 jit_solution(1827544013982923362)
XLA Ops:
  0.6 0.7 fusion.3
  1.3 0.7 fusion.6
  5.8 3.2 %stack.53.scal_ref = f32[27]{0:T(128)} concatenate(f32[1]{0:T(128)} %bitcast, f32[1]{0:T(128)} %bitcast.1, f32[1]{0:T(128)} %bitcast.2, f32[1]{0:T(128)} %bitcast.3, f32[1]{0:T(128)} %bitcast.6, f32[1]{0:T(128)S(6)} %div.60, f32[1]{0:T(128)} %constant.24.clone.1, f32[1]{0:T(128)} %bitcast.7, f32[1]{0:T(128)S(6)} %div.60, f32[1]{0:T(128)} %bitcast.8, f32[1]{0:T(128)} %bitcast.9, ...), dimensions={0} | concatenate | bytes 216 | tf_op jit(solution)/shard_map/stack | solution.py:496
  9.0 1.3 %reshape_squeeze.3 = f32[2,2,6,48,48]{4,3,1,2,0:T(8,128)S(1)} reshape(f32[1,2,2,6,2304]{4,2,3,1,0:T(2,128)} %param.11) | data formatting | bytes 442368 | tf_op jit(solution)/shard_map/reshape;squeeze | solution.py:511
  10.3 0.5 copy.32
  10.8 0.3 reshape.46
  11.1 0.1 fusion.5
  11.3 0.0 copy-start
  11.3 0.8 pad_maximum_fusion.1.packed_ref
  12.1 0.1 copy-done
  12.2 0.1 reshape.48
  12.3 0.1 copy.33
  12.4 0.0 copy-start.3
  12.4 0.1 reshape.49
  12.5 0.0 copy-start.1
  12.5 0.0 copy-start.2
  12.5 0.6 pad.5.pot_ref
  13.2 0.0 copy-done.3
  13.2 0.2 copy-done.1
  13.4 0.1 copy-done.2
  13.4 1.4 %fusion.2 = (bf16[128,128]{1,0:T(8,128)(2,1)S(1)}, bf16[128,128]{1,0:T(8,128)(2,1)S(1)}) fusion(f32[128,128]{1,0:T(8,128)S(1)} %copy-done.1, f32[128,128]{1,0:T(8,128)S(1)} %copy-done.2, f32[128,128]{1,0:T(8,128)S(1)} %copy-done.3, f32[]{:T(128)} %bitcast.21, f32[]{:T(128)} %bitcast.20), kind=kLoop, calls=%fused_computation.9 | loop fusion | flops 131072 | bytes 262152 | tf_op jit(solution)/shard_map/convert_element_type | solution.py:502
  14.8 0.7 fusion.1.mat_ref
  15.4 105.5 %cheb.1 = (f32[2,6,48,128]{3,2,1,0:T(8,128)}, f32[2,8,128]{2,1,0:T(8,128)}, f32[8,128]{1,0:T(8,128)}) custom-call(f32[27]{0:T(128)} %stack.53.scal_ref, f32[2,9,24,128]{3,2,1,0:T(8,128)} %pad_maximum_fusion.1.packed_ref, f32[3,48,128]{2,1,0:T(8,128)} %pad.5.pot_ref, bf16[256,256]{1,0:T(8,128)(2,1)} %fusion.1.mat_ref), custom_call_target="tpu_custom_call" | custom-call | tf_op jit(solution)/shard_map/cheb/pallas_call | solution.py:524
  121.0 1.3 %reshape.50 = f32[2,6,48,2,48]{4,3,2,1,0:T(2,128)S(1)} reshape(f32[2,6,48,96]{3,2,1,0:T(8,128)} %bitcast.42) | data formatting | bytes 442368 | tf_op jit(solution)/shard_map/reshape | solution.py:555
  122.3 1.1 reshape.51
  123.5 1.3 %slice_reduce_fusion = f32[2]{0:T(128)} fusion(f32[2,8,128]{2,1,0:T(8,128)} %get-tuple-element.7), kind=kLoop, calls=%fused_computation.11 | loop fusion | bytes 16 | tf_op jit(solution)/shard_map/slice | solution.py:557
  124.8 1.2 slice.73
  (4 shorter events, 0.1 us)
Async XLA Ops:
  11.3 0.9 copy-start
  12.4 0.8 copy-start.3
  12.5 0.8 copy-start.1
  12.5 0.9 copy-start.2
where the time goes:
time: 126 us
  Pallas kernels  106 us (84%)
  local copies, waits for them, and re-layouts  12.4 us (10%)
  between operations  4.54 us (4%)
  other arithmetic  3.55 us (3%)
    pallas_call x1, Pallas kernels, per_device(): pl.pallas_call(functools.partial(kernel, n, members_k), name='cheb', out_...  106 us
    another operation x1, local copies, waits for them, and re-layouts, per_device(): scalars = jnp.stack(scalars)  3.17 us

commit v1 on v0

--- a/solution.py
+++ b/solution.py
@@ -63,14 +63,22 @@
 def kernel(
     n,
     members_k,
-    scal_ref,
+    table_ref,
+    kweight_ref,
+    lowest_ref,
+    cut_ref,
+    upper_ref,
+    fermi_ref,
     packed_ref,
     pot_ref,
-    mat_ref,
+    parts_ref,
     out_ref,
     energy_ref,
     total_ref,
-    field,
+    field_0,
+    field_1,
+    field_2,
+    mat_ref,
     potential,
     gathered,
     gathered_pot,
@@ -147,15 +155,54 @@
         signed = jnp.where(used, jnp.where(first, -sine, sine), 0.0)
         return cosine * v + signed * other
 
-    cos_x, sin_x = scal_ref[0], scal_ref[1]
-    cos_y, sin_y = scal_ref[2], scal_ref[3]
-
-    def put(slot, plane, t, v):
-        field[slot, plane, pl.ds(PAD + 8 * t, 8), :] = v
+    def spread(scalar):
+        return jnp.full((8, LANES), scalar)
+
+    def phase(d):
+        numerator = spread(table_ref[0, d])
+        cosine, sine = jnp.ones((8, LANES), jnp.float32), zero
+        for i in range(1, PHASE_DIVISOR):
+            here = numerator == i
+            angle = 2.0 * np.pi * i / PHASE_DIVISOR
+            cosine = jnp.where(here, float(np.cos(angle)), cosine)
+            sine = jnp.where(here, float(np.sin(angle)), sine)
+        return cosine, sine
+
+    cos_x, sin_x = phase(0)
+    cos_y, sin_y = phase(1)
+    cos_z, sin_z = phase(2)
+    low_end, cut_end, high_end = (spread(r[0]) for r in (lowest_ref, cut_ref, upper_ref))
+    half_width = (high_end - cut_end) / 2.0
+    centre = (high_end + cut_end) / 2.0
+    first_sigma = half_width / (low_end - centre)
+    sigma = first_sigma
+    recurrence = [(first_sigma / half_width, None)]
+    for degree in range(1, DEGREE):
+        next_sigma = 1.0 / (2.0 / first_sigma - sigma)
+        recurrence.append((2.0 * next_sigma / half_width, sigma * next_sigma))
+        sigma = next_sigma
+
+    for r in range(LANES // 16):
+        rows = pl.ds(16 * r, 16)
+        cosine = jnp.concatenate([cos_z, cos_z], axis=0)
+        sine = jnp.concatenate([sin_z, sin_z], axis=0)
+        entry = parts_ref[0, rows, :] + cosine * parts_ref[1, rows, :] + sine * parts_ref[2, rows, :]
+        high = entry.astype(jnp.bfloat16)
+        rest = (entry - high.astype(jnp.float32)).astype(jnp.bfloat16)
+        lower = pl.ds(LANES + 16 * r, 16)
+        mat_ref[rows, pl.ds(0, LANES)] = high
+        mat_ref[rows, pl.ds(LANES, LANES)] = rest
+        mat_ref[lower, pl.ds(0, LANES)] = high
+        mat_ref[lower, pl.ds(LANES, LANES)] = jnp.zeros_like(high)
+
+    fields = (field_0, field_1, field_2)
+
+    def put(field, plane, t, v):
+        field[plane, pl.ds(PAD + 8 * t, 8), :] = v
         if t == 0:
-            field[slot, plane, pl.ds(PAD + SIDE, 8), :] = turn(v, cos_y, sin_y)
+            field[plane, pl.ds(PAD + SIDE, 8), :] = turn(v, cos_y, sin_y)
         if t == TILES - 1:
-            field[slot, plane, pl.ds(0, 8), :] = turn(v, cos_y, -sin_y)
+            field[plane, pl.ds(0, 8), :] = turn(v, cos_y, -sin_y)
 
     def unpack(load, slab):
         place = lax.rem(slab - 2 * chip + home + blocks, blocks)
@@ -177,12 +224,18 @@
                             piece = pltpu.roll(load(3 * g + q, r), 32 + 32 * q, 1)
                             inside = (lane >= 32 * q) & (lane < 32 * q + 32)
                             v = jnp.where(inside, piece, v)
-                    put(0, base + plane, half * (HALF // 8) + r, change(v))
-
-        sine = jnp.where(wrapped_low, -sin_x, sin_x)
-        sine = jnp.where(wrapped_low | wrapped_high, sine, 0.0)
-        cosine = jnp.where(wrapped_low | wrapped_high, cos_x, 1.0)
-        emit(lambda v: turn(v, cosine, sine))
+                    put(field_0, base + plane, half * (HALF // 8) + r, change(v))
+
+        wrapped = wrapped_low | wrapped_high
+
+        @pl.when(wrapped)
+        def _():
+            way = jnp.where(wrapped_low, -1.0, 1.0)
+            emit(lambda v: turn(v, cos_x, way * sin_x))
+
+        @pl.when(jnp.logical_not(wrapped))
+        def _():
+            emit(lambda v: v)
 
     def unpack_pot(load, slab):
         place = lax.rem(slab - 2 * chip + home + blocks, blocks)
@@ -294,72 +347,72 @@
 
     lax.fori_loop(0, chips, other_pot, 0)
 
-    def wrap_planes(slot):
+    def wrap_planes(field):
         def one(i, carry):
-            for t in range(ROWS // 8):
-                rows = pl.ds(8 * t, 8)
-                low = field[slot, blocks * planes + i, rows, :]
-                field[slot, i, rows, :] = turn(low, cos_x, -sin_x)
-                high = field[slot, planes + i, rows, :]
-                field[slot, planes + blocks * planes + i, rows, :] = turn(high, cos_x, sin_x)
+            tiles = [pl.ds(8 * t, 8) for t in range(ROWS // 8)]
+            lows = [field[blocks * planes + i, rows, :] for rows in tiles]
+            highs = [field[planes + i, rows, :] for rows in tiles]
+            lows = [turn(v, cos_x, -sin_x) for v in lows]
+            highs = [turn(v, cos_x, sin_x) for v in highs]
+            for rows, low, high in zip(tiles, lows, highs):
+                field[i, rows, :] = low
+                field[planes + blocks * planes + i, rows, :] = high
             return carry
 
         lax.fori_loop(0, planes, one, 0)
 
-    wrap_planes(0)
+    wrap_planes(field_0)
     weights = [-0.5 * c for c in coefficients]
 
-    def step(m, carry):
-        now = lax.rem(m - 1, 3)
-        new = lax.rem(m, 3)
-        old = jnp.where(m == 1, now, lax.rem(m + 1, 3))
-        gain, centre, back = scal_ref[3 * m + 1], scal_ref[3 * m + 2], scal_ref[3 * m + 3]
-        low = jnp.maximum(0, m - (DEGREE + 1) + home)
-
-        def block(k, inner):
-            base = k * planes
-            middle = [field[now, base + planes + p, pl.ds(PAD, SIDE), :] for p in range(planes)]
-            rows = jnp.concatenate(middle, axis=0)
-            high = rows.astype(jnp.bfloat16)
-            rest = (rows - high.astype(jnp.float32)).astype(jnp.bfloat16)
-            both = jnp.concatenate([high, rest], axis=1)
-            third = jnp.dot(both, mat_ref[...], preferred_element_type=jnp.float32)
-            third = third[:, :LANES] + third[:, LANES:]
-            for t in range(TILES):
-                window = [
-                    field[now, base + i, pl.ds(PAD + 8 * t, 8), :] for i in range(3 * planes)
-                ]
-                for p in range(planes):
-                    centre_value = window[planes + p]
-                    total = third[p * SIDE + 8 * t : p * SIDE + 8 * t + 8, :]
-                    total = total + centre_value * (
-                        potential[base + p, pl.ds(8 * t, 8), :] - centre
-                    )
-                    for j in range(1, REACH + 1):
-                        around = window[planes + p + j] + window[planes + p - j]
-                        above = field[now, base + planes + p, pl.ds(PAD + 8 * t + j, 8), :]
-                        below = field[now, base + planes + p, pl.ds(PAD + 8 * t - j, 8), :]
-                        total = total + weights[j] * (around + (above + below))
-                    previous = field[old, base + planes + p, pl.ds(PAD + 8 * t, 8), :]
-                    put(new, base + planes + p, t, gain * total - back * previous)
-            return inner
+    def apply(m, k):
+        field = fields[(m - 1) % 3]
+        base = k * planes
+        middle = [field[base + planes + p, pl.ds(PAD, SIDE), :] for p in range(planes)]
+        rows = jnp.concatenate(middle, axis=0)
+        high = rows.astype(jnp.bfloat16)
+        rest = (rows - high.astype(jnp.float32)).astype(jnp.bfloat16)
+        both = jnp.concatenate([high, rest], axis=1)
+        third = jnp.dot(both, mat_ref[...], preferred_element_type=jnp.float32)
+        third = third[:, :LANES] + third[:, LANES:]
+        for t in range(TILES):
+            tile = pl.ds(PAD + 8 * t, 8)
+            window = [field[base + i, tile, :] for i in range(3 * planes)]
+            for p in range(planes):
+                value = window[planes + p]
+                total = third[p * SIDE + 8 * t : p * SIDE + 8 * t + 8, :]
+                shift = potential[base + p, pl.ds(8 * t, 8), :]
+                if m <= DEGREE:
+                    shift = shift - centre
+                total = total + value * shift
+                for j in range(1, REACH + 1):
+                    around = window[planes + p + j] + window[planes + p - j]
+                    above = field[base + planes + p, pl.ds(PAD + 8 * t + j, 8), :]
+                    below = field[base + planes + p, pl.ds(PAD + 8 * t - j, 8), :]
+                    total = total + weights[j] * (around + (above + below))
+                yield base + planes + p, t, tile, value, total
+
+    for m in range(1, DEGREE + 1):
+        gain, back = recurrence[m - 1]
+        low = max(0, m - (DEGREE + 1) + home)
+
+        def block(k, carry, m=m, gain=gain, back=back):
+            for plane, t, tile, _, total in apply(m, k):
+                following = gain * total
+                if back is not None:
+                    following = following - back * fields[(m + 1) % 3][plane, tile, :]
+                put(fields[m % 3], plane, t, following)
+            return carry
 
         lax.fori_loop(low, blocks - low, block, 0)
-
-        @pl.when(m - DEGREE + home <= 0)
-        def _():
-            wrap_planes(new)
-
-        return carry
-
-    lax.fori_loop(1, DEGREE + 2, step, 0)
-    slot, applied = DEGREE % 3, (DEGREE + 1) % 3
+        if m - DEGREE + home <= 0:
+            wrap_planes(fields[m % 3])
+    final = fields[DEGREE % 3]
 
     mine = planes + (home + core) * planes
     theirs = planes + (home + 1 - core) * planes
     body = pl.ds(PAD, SIDE)
     swap = remote(
-        field.at[slot, pl.ds(theirs, planes), body, :],
+        final.at[pl.ds(theirs, planes), body, :],
         out_ref.at[core],
         swap_sem.at[0],
         swap_sem.at[1],
@@ -367,16 +420,15 @@
     )
     swap.start()
 
-    def sums(i, carry):
-        top, bottom = carry
-        plane = planes + home * planes + i
-        for t in range(TILES):
-            f = field[slot, plane, pl.ds(PAD + 8 * t, 8), :]
-            top = top + f * field[applied, plane, pl.ds(PAD + 8 * t, 8), :]
-            bottom = bottom + f * f
-        return top, bottom
-
-    top, bottom = lax.fori_loop(0, 2 * planes, sums, (zero, zero))
+    def sums(k, carry):
+        tops, bottoms = list(carry[0]), list(carry[1])
+        for plane, t, _, value, total in apply(DEGREE + 1, k):
+            tops[t % 2] = tops[t % 2] + value * total
+            bottoms[t % 2] = bottoms[t % 2] + value * value
+        return tuple(tops), tuple(bottoms)
+
+    tops, bottoms = lax.fori_loop(home, blocks - home, sums, ((zero, zero), (zero, zero)))
+    top, bottom = tops[0] + tops[1], bottoms[0] + bottoms[1]
     part[me, 0] = jnp.broadcast_to(jnp.sum(top, keepdims=True), (8, LANES))
     part[me, 1] = jnp.broadcast_to(jnp.sum(bottom, keepdims=True), (8, LANES))
 
@@ -389,13 +441,13 @@
         reduction(d).start()
     for i in range(planes):
         for t in range(TILES):
-            out_ref[core, i, pl.ds(8 * t, 8), :] = field[slot, mine + i, pl.ds(PAD + 8 * t, 8), :]
+            out_ref[core, i, pl.ds(8 * t, 8), :] = final[mine + i, pl.ds(PAD + 8 * t, 8), :]
     for d in range(1, n):
         source = lax.rem(me + d, n)
         remote(
             part.at[source], part.at[source], send_red.at[d], recv_red.at[source], source
         ).wait_recv()
-    kweight, fermi = scal_ref[3 * DEGREE + 7], scal_ref[3 * DEGREE + 8]
+    kweight, fermi = kweight_ref[0], fermi_ref[0]
     term = zero
     for b in range(2):
         numerator, denominator = zero, zero
@@ -478,35 +530,7 @@
     n = lax.axis_size("grid")
     members_k = lax.axis_size("kpt")
     planes = bands.shape[3]
-    angles = 2.0 * jnp.pi * table[0].astype(jnp.float32) / PHASE_DIVISOR
-    cosines, sines = jnp.cos(angles), jnp.sin(angles)
-
-    half_width = (upper[0] - cut[0]) / 2.0
-    centre = (upper[0] + cut[0]) / 2.0
-    first_sigma = half_width / (lowest[0] - centre)
-    sigma = first_sigma
-    nothing = jnp.zeros((), jnp.float32)
-    scalars = [cosines[0], sines[0], cosines[1], sines[1]]
-    scalars += [first_sigma / half_width, centre, nothing]
-    for degree in range(1, DEGREE):
-        next_sigma = 1.0 / (2.0 / first_sigma - sigma)
-        scalars += [2.0 * next_sigma / half_width, centre, sigma * next_sigma]
-        sigma = next_sigma
-    scalars += [nothing + 1.0, nothing, nothing, kweight[0], fermi[0]]
-    scalars = jnp.stack(scalars)
-
-    plain, cosine, sine = third_parts()
-    matrix = plain + cosines[2] * cosine + sines[2] * sine
-    rounded = lax.reduce_precision(matrix, 8, 7)
-    high = rounded.astype(jnp.bfloat16)
-    rest = (matrix - rounded).astype(jnp.bfloat16)
-    matrix = jnp.concatenate(
-        [
-            jnp.concatenate([high, rest], axis=1),
-            jnp.concatenate([high, jnp.zeros_like(high)], axis=1),
-        ],
-        axis=0,
-    )
+    parts = jnp.asarray(np.stack(third_parts()))
 
     waves = bands[0].reshape(2, 2, planes, SIDE, SIDE).transpose(1, 2, 3, 0, 4)
     waves = waves.reshape(2, 2 * planes, HALF, USED)
@@ -529,10 +553,13 @@
             jax.ShapeDtypeStruct((2, 8, LANES), jnp.float32),
             jax.ShapeDtypeStruct((8, LANES), jnp.float32),
         ),
-        in_specs=[pl.BlockSpec(memory_space=pltpu.SMEM), vmem, vmem, vmem],
+        in_specs=[pl.BlockSpec(memory_space=pltpu.SMEM)] * 6 + [vmem] * 3,
         out_specs=(vmem, vmem, vmem),
         scratch_shapes=[
-            pltpu.VMEM((3, total_planes + 2 * planes, ROWS, LANES), jnp.float32),
+            pltpu.VMEM((total_planes + 2 * planes, ROWS, LANES), jnp.float32),
+            pltpu.VMEM((total_planes + 2 * planes, ROWS, LANES), jnp.float32),
+            pltpu.VMEM((total_planes + 2 * planes, ROWS, LANES), jnp.float32),
+            pltpu.VMEM((2 * LANES, 2 * LANES), jnp.bfloat16),
             pltpu.VMEM((total_planes, SIDE, LANES), jnp.float32),
             pltpu.VMEM((n, 9, HALF, LANES), jnp.float32),
             pltpu.VMEM((n, planes // 2, SIDE, LANES), jnp.float32),
@@ -551,7 +578,7 @@
         compiler_params=pltpu.CompilerParams(
             collective_id=0, has_side_effects=True, vmem_limit_bytes=56 * 1024 * 1024
         ),
-    )(scalars, packed, pairs, matrix)
+    )(table, kweight, lowest, cut, upper, fermi, packed, pairs, parts)
     filtered = out[..., :USED].reshape(2, planes, SIDE, 2, SIDE).transpose(3, 0, 1, 2, 4)
     filtered = filtered.reshape(1, 2, 2, planes, SIDE * SIDE)
     return filtered, energy[:, 0, 0][None], total[0, :1]

time: 126 us -> 71.6 us (0.57)
  Pallas kernels: 106 us -> 58.2 us
  local copies, waits for them, and re-layouts: 12.4 us -> 8.25 us
  other arithmetic: 3.55 us -> 0.83 us
    pallas_call x1, Pallas kernels: 106 us -> 58.2 us  [per_device(): pl.pallas_call(functools.partial(kernel, n, members_k), name='cheb', out_...]
    another operation x2 -> x0, local copies, waits for them, and re-layouts: 3.17 us -> none  [the longest x1 3.17 us: per_device(): scalars = jnp.stack(scalars)]
    convert_element_type x1 -> x0, other arithmetic: 1.36 us -> none  [per_device(): rest = (matrix - rounded).astype(jnp.bfloat16)]
where the time goes in v1:
time: 71.6 us; the launch traced here: 71.2 us
  Pallas kernels  58.2 us (81%)
  local copies, waits for them, and re-layouts  8.25 us (12%)
  between operations  3.97 us (6%)
  other arithmetic  0.83 us (1%)
    pallas_call x1, Pallas kernels, per_device(): pl.pallas_call(functools.partial(kernel, n, members_k), name='cheb', out_...  58.2 us
    slice x2, local copies, waits for them, and re-layouts, per_device(): return (filtered, energy[:, 0, 0][None], total[0, :1])  2.49 us
    another operation x2, local copies, waits for them, and re-layouts, per_device(): waves = bands[0].reshape(2, 2, planes, SIDE, SIDE).transpose(1, 2, 3, 0, 4)  1.79 us

profile of v1, /device:TPU:0, one launch (start us, length us, event | category | flops | bytes accessed | tf_op | source)
XLA Modules:
  0.0 71.2 jit_solution(9591200044052813113)
XLA Ops:
  0.6 1.3 %reshape_squeeze.3 = f32[2,2,6,48,48]{4,3,1,2,0:T(8,128)S(1)} reshape(f32[1,2,2,6,2304]{4,2,3,1,0:T(2,128)} %param.9) | data formatting | bytes 442368 | tf_op jit(solution)/shard_map/reshape;squeeze | solution.py:535
  2.0 0.5 copy.30
  2.4 0.3 reshape.25
  2.8 0.1 fusion
  2.9 0.0 copy-start
  2.9 0.8 %pad_maximum_fusion.1.packed_ref = f32[2,9,24,128]{3,2,1,0:T(8,128)} fusion(f32[2,9,24,32]{3,2,1,0:T(8,128)S(1)} %bitcast.21, f32[2,9,24,96]{3,2,1,0:T(8,128)S(1)} %slice.32), kind=kLoop, calls=%fused_computation.2 | loop fusion | flops 55296 | bytes 442368 | tf_op jit(solution)/shard_map/concatenate | solution.py:539
  3.8 0.1 copy-done
  3.8 0.1 reshape.27
  3.9 0.1 copy.31
  4.0 0.1 reshape.28
  4.2 0.7 pad.4.pot_ref
  8.1 58.2 %cheb.1 = (f32[2,6,48,128]{3,2,1,0:T(8,128)}, f32[2,8,128]{2,1,0:T(8,128)}, f32[8,128]{1,0:T(8,128)}) custom-call(s32[1,3]{1,0:T(1,128)} %table_ref.1, f32[1]{0:T(128)S(6)} %copy.32.kweight_ref, f32[1]{0:T(128)S(6)} %copy.33.lowest_ref, f32[1]{0:T(128)S(6)} %copy.34.cut_ref, f32[1]{0:T(128)S(6)} %copy.35.upper_ref, f32[1]{0:T(128)S(6)} %copy.36.fermi_ref, ...), custom_call_target="tpu_custom_call" | custom-call | tf_op jit(solution)/shard_map/cheb/pallas_call | solution.py:548
  66.2 1.3 %reshape.29 = f32[2,6,48,2,48]{4,3,2,1,0:T(2,128)S(1)} reshape(f32[2,6,48,96]{3,2,1,0:T(8,128)} %bitcast.23) | data formatting | bytes 442368 | tf_op jit(solution)/shard_map/reshape | solution.py:582
  67.6 1.1 %reshape.30 = f32[1,2,2,6,2304]{4,2,3,1,0:T(2,128)} reshape(f32[2,2,6,48,48]{4,3,1,2,0:T(8,128)S(1)} %copy.27) | data formatting | bytes 442368 | tf_op jit(solution)/shard_map/reshape | solution.py:583
  68.7 1.2 %slice.31 = f32[1,1]{1,0:T(1,128)} slice(f32[8,128]{1,0:T(8,128)} %get-tuple-element.8), slice={[0:1], [0:1]} | slice | bytes 8 | tf_op jit(solution)/shard_map/slice | solution.py:584
  69.9 1.3 %slice_reduce_fusion = f32[2]{0:T(128)} fusion(f32[2,8,128]{2,1,0:T(8,128)} %get-tuple-element.7), kind=kLoop, calls=%fused_computation.4 | loop fusion | bytes 16 | tf_op jit(solution)/shard_map/slice | solution.py:584
  (3 shorter events, 0.1 us)
Async XLA Ops:
  2.9 0.9 %copy-start = (f32[6,2304]{1,0:T(8,128)S(1)}, f32[6,2304]{1,0:T(8,128)}, u32[]{:S(2)}) copy-start(f32[6,2304]{1,0:T(8,128)} %param.10) | copy-start | bytes 165892
